TPU v7x, 16 devices: a whole 2x2x2 slice. The times are simulated.
16 devices in a mesh: dp: 1, tp: 16 (over x, y, z, core).
Axes of the slice: x: 2, y: 2, z: 2, core: 2. Of those that a mesh axis runs over, the one named last changes fastest.
Arguments:
- x: bfloat16 [2560, 7168], P(('dp', 'tp'))
- dy: bfloat16 [2560, 7168], P(('dp', 'tp'))
- gate: bfloat16 [2560, 20480], P('dp', 'tp')
- up: bfloat16 [2560, 20480], P('dp', 'tp')
- w_gate: bfloat16 [7168, 20480], P(None, 'tp')
- w_up: bfloat16 [7168, 20480], P(None, 'tp')
- w_down: bfloat16 [20480, 7168], P('tp')
Outputs:
- output 1: bfloat16 [2560, 7168], P(('dp', 'tp'))
- output 2: bfloat16 [7168, 20480], P('dp', 'tp')
- output 3: bfloat16 [7168, 20480], P('dp', 'tp')
- output 4: bfloat16 [20480, 7168], P(('dp', 'tp'))
All inputs are finite; a program needn't handle non-finite values.
Results may differ from a plain program's by a relative error of at most 0.012.
Values are sent between devices in bfloat16 or wider.
A program may use at most 2 GiB of HBM per device.

v0:
```python
import jax
import jax.numpy as jnp


def act(gate, up):
    return jax.nn.silu(gate) * up


def solution(mesh):
    def step(x, dy, gate, up, w_gate, w_up, w_down):
        hidden, back = jax.vjp(act, gate.astype(jnp.float32), up.astype(jnp.float32))
        d_hidden = jnp.dot(dy, w_down.T, preferred_element_type=jnp.float32)
        d_gate, d_up = (g.astype(jnp.bfloat16) for g in back(d_hidden))
        dx = jnp.dot(d_gate, w_gate.T) + jnp.dot(d_up, w_up.T)
        groups = mesh.shape["dp"]

        def by_group(a, b):
            a, b = (t.reshape(groups, -1, t.shape[-1]) for t in (a, b))
            product = jnp.einsum("gta,gtb->gab", a, b, preferred_element_type=jnp.float32)
            return product.astype(jnp.bfloat16).reshape(-1, b.shape[-1])

        return dx, by_group(x, d_gate), by_group(x, d_up), by_group(hidden.astype(jnp.bfloat16), dy)

    return step
```

profile of v0, /device:TPU:0, one launch (start us, length us, event | category | flops | bytes accessed | tf_op | source)
XLA Modules:
  0.0 1761.2 jit_solution(17330512021399278826)
XLA Ops:
  8.7 145.9 %all-gather.7.cloned.1.call-done = bf16[2560,7168]{1,0:T(8,128)(2,1)} async-done(((bf16[160,7168]{1,0:T(8,128)(2,1)}), bf16[2560,7168]{1,0:T(8,128)(2,1)}) %all-gather.7.cloned.1.call-update) | async-done | bytes 36700176 | tf_op args[1]
  154.6 64.6 %fusion.40 = (bf16[2560,1280]{1,0:T(8,128)(2,1)}, bf16[2560,1280]{1,0:T(8,128)(2,1)}) fusion(bf16[2560,1280]{1,0:T(8,128)(2,1)} %param.7, bf16[2560,1280]{1,0:T(8,128)(2,1)} %param.6, bf16[2560,7168]{1,0:T(8,128)(2,1)} %all-gather.7.cloned.1.call-done, bf16[1280,7168]{1,0:T(8,128)(2,1)} %param.5), kind=kOutput, calls=%fused_computation.65 | convolution fusion | flops 47028633600 | bytes 81264640 | tf_op jit(solution)/dot_general | solution.py:12
  219.2 645.3 %while.5 = (bf16[2560,1280]{1,0:T(8,128)(2,1)}, bf16[7168,1280]{1,0:T(8,128)(2,1)}, bf16[160,7168]{1,0:T(8,128)(2,1)}, bf16[160,7168]{1,0:T(8,128)(2,1)}, u32[]{...) while((bf16[2560,1280]{1,0:T(8,128)(2,1)}, ...), condition=%wide.windowed_dot_general_cond_rs.1.clone, body=%wide.windowed_dot_general_body_rs.1.clone.sunk | while | flops 11754209280 | bytes 141558400 | solution.py:14
  234.9 58.0 %collective-permute-done.5 = bf16[160,7168]{1,0:T(8,128)(2,1)} collective-permute-done((bf16[160,7168]{1,0:T(8,128)(2,1)}, bf16[160,7168]{1,0:T(8,128)(2,1)}, u32[]{:S(2)}, u32[]{:S(2)}) %collective-permute-start.5) | collective-permute-done | bytes 2293792 | tf_op jit(solution)/dot_general | solution.py:14
  366.3 55.3 %collective-permute-start.4 = (bf16[160,7168]{1,0:T(8,128)(2,1)}, bf16[160,7168]{1,0:T(8,128)(2,1)}, u32[]{:S(2)}, u32[]{:S(2)}) collective-permute-start(bf16[160,7168]{1,0:T(8,128)(2,1)} %broadcast_select_fusion.10), channel_id=10, source_target_pairs={{0,1},{1,2},{2,3},{3,4},{4,5},{5,6},{6,7},{7,8},{8,9},{9,10},{10,1... | collective-permute-start | bytes 6881288 | tf_op jit(solution)/dot_general | solution.py:14
  457.7 45.0 %collective-permute-start.6 = (bf16[160,7168]{1,0:T(8,128)(2,1)}, bf16[160,7168]{1,0:T(8,128)(2,1)}, u32[]{:S(2)}, u32[]{:S(2)}) collective-permute-start(bf16[160,7168]{1,0:T(8,128)(2,1)} %get-tuple-element.160), channel_id=12, source_target_pairs={{0,1},{1,2},{2,3},{3,4},{4,5},{5,6},{6,7},{7,8},{8,9},{9,10},{10,1... | collective-permute-start | bytes 6881288 | tf_op jit(solution)/dot_general | solution.py:14
  542.3 44.8 %collective-permute-start.4 = (bf16[160,7168]{1,0:T(8,128)(2,1)}, bf16[160,7168]{1,0:T(8,128)(2,1)}, u32[]{:S(2)}, u32[]{:S(2)}) collective-permute-start(bf16[160,7168]{1,0:T(8,128)(2,1)} %broadcast_select_fusion.10), channel_id=10, source_target_pairs={{0,1},{1,2},{2,3},{3,4},{4,5},{5,6},{6,7},{7,8},{8,9},{9,10},{10,1... | collective-permute-start | bytes 6881288 | tf_op jit(solution)/dot_general | solution.py:14
  623.1 45.0 %collective-permute-start.6 = (bf16[160,7168]{1,0:T(8,128)(2,1)}, bf16[160,7168]{1,0:T(8,128)(2,1)}, u32[]{:S(2)}, u32[]{:S(2)}) collective-permute-start(bf16[160,7168]{1,0:T(8,128)(2,1)} %get-tuple-element.160), channel_id=12, source_target_pairs={{0,1},{1,2},{2,3},{3,4},{4,5},{5,6},{6,7},{7,8},{8,9},{9,10},{10,1... | collective-permute-start | bytes 6881288 | tf_op jit(solution)/dot_general | solution.py:14
  707.7 44.8 %collective-permute-start.4 = (bf16[160,7168]{1,0:T(8,128)(2,1)}, bf16[160,7168]{1,0:T(8,128)(2,1)}, u32[]{:S(2)}, u32[]{:S(2)}) collective-permute-start(bf16[160,7168]{1,0:T(8,128)(2,1)} %broadcast_select_fusion.10), channel_id=10, source_target_pairs={{0,1},{1,2},{2,3},{3,4},{4,5},{5,6},{6,7},{7,8},{8,9},{9,10},{10,1... | collective-permute-start | bytes 6881288 | tf_op jit(solution)/dot_general | solution.py:14
  788.6 45.0 %collective-permute-start.6 = (bf16[160,7168]{1,0:T(8,128)(2,1)}, bf16[160,7168]{1,0:T(8,128)(2,1)}, u32[]{:S(2)}, u32[]{:S(2)}) collective-permute-start(bf16[160,7168]{1,0:T(8,128)(2,1)} %get-tuple-element.160), channel_id=12, source_target_pairs={{0,1},{1,2},{2,3},{3,4},{4,5},{5,6},{6,7},{7,8},{8,9},{9,10},{10,1... | collective-permute-start | bytes 6881288 | tf_op jit(solution)/dot_general | solution.py:14
  888.5 608.6 %while.4 = (bf16[2560,1280]{1,0:T(8,128)(2,1)}, bf16[7168,1280]{1,0:T(8,128)(2,1)}, bf16[160,7168]{1,0:T(8,128)(2,1)S(1)}, bf16[160,7168]{1,0:T(8,128)(2,1)}, u3...) while((bf16[2560,1280]{1,0:T(8,128)(2,1)}, ...), condition=%wide.windowed_dot_general_cond_rs.clone, body=%wide.windowed_dot_general_body_rs.clone.sunk | while | flops 11754209280 | bytes 150733472 | solution.py:14
  927.1 48.3 %collective-permute-start.2 = (bf16[160,7168]{1,0:T(8,128)(2,1)}, bf16[160,7168]{1,0:T(8,128)(2,1)}, u32[]{:S(2)}, u32[]{:S(2)}) collective-permute-start(bf16[160,7168]{1,0:T(8,128)(2,1)} %get-tuple-element.151), channel_id=6, source_target_pairs={{0,1},{1,2},{2,3},{3,4},{4,5},{5,6},{6,7},{7,8},{8,9},{9,10},{10,1... | collective-permute-start | bytes 6881288 | tf_op jit(solution)/dot_general | solution.py:14
  1012.5 45.5 %collective-permute-start = (bf16[160,7168]{1,0:T(8,128)(2,1)}, bf16[160,7168]{1,0:T(8,128)(2,1)}, u32[]{:S(2)}, u32[]{:S(2)}) collective-permute-start(bf16[160,7168]{1,0:T(8,128)(2,1)} %broadcast_select_fusion.8), channel_id=4, source_target_pairs={{0,1},{1,2},{2,3},{3,4},{4,5},{5,6},{6,7},{7,8},{8,9},{9,10},{10,1... | collective-permute-start | bytes 6881288 | tf_op jit(solution)/dot_general | solution.py:14
  1092.6 46.6 %collective-permute-start.2 = (bf16[160,7168]{1,0:T(8,128)(2,1)}, bf16[160,7168]{1,0:T(8,128)(2,1)}, u32[]{:S(2)}, u32[]{:S(2)}) collective-permute-start(bf16[160,7168]{1,0:T(8,128)(2,1)} %get-tuple-element.151), channel_id=6, source_target_pairs={{0,1},{1,2},{2,3},{3,4},{4,5},{5,6},{6,7},{7,8},{8,9},{9,10},{10,1... | collective-permute-start | bytes 6881288 | tf_op jit(solution)/dot_general | solution.py:14
  1176.3 45.5 %collective-permute-start = (bf16[160,7168]{1,0:T(8,128)(2,1)}, bf16[160,7168]{1,0:T(8,128)(2,1)}, u32[]{:S(2)}, u32[]{:S(2)}) collective-permute-start(bf16[160,7168]{1,0:T(8,128)(2,1)} %broadcast_select_fusion.8), channel_id=4, source_target_pairs={{0,1},{1,2},{2,3},{3,4},{4,5},{5,6},{6,7},{7,8},{8,9},{9,10},{10,1... | collective-permute-start | bytes 6881288 | tf_op jit(solution)/dot_general | solution.py:14
  1256.4 46.6 %collective-permute-start.2 = (bf16[160,7168]{1,0:T(8,128)(2,1)}, bf16[160,7168]{1,0:T(8,128)(2,1)}, u32[]{:S(2)}, u32[]{:S(2)}) collective-permute-start(bf16[160,7168]{1,0:T(8,128)(2,1)} %get-tuple-element.151), channel_id=6, source_target_pairs={{0,1},{1,2},{2,3},{3,4},{4,5},{5,6},{6,7},{7,8},{8,9},{9,10},{10,1... | collective-permute-start | bytes 6881288 | tf_op jit(solution)/dot_general | solution.py:14
  1340.1 45.5 %collective-permute-start = (bf16[160,7168]{1,0:T(8,128)(2,1)}, bf16[160,7168]{1,0:T(8,128)(2,1)}, u32[]{:S(2)}, u32[]{:S(2)}) collective-permute-start(bf16[160,7168]{1,0:T(8,128)(2,1)} %broadcast_select_fusion.8), channel_id=4, source_target_pairs={{0,1},{1,2},{2,3},{3,4},{4,5},{5,6},{6,7},{7,8},{8,9},{9,10},{10,1... | collective-permute-start | bytes 6881288 | tf_op jit(solution)/dot_general | solution.py:14
  1420.2 46.6 %collective-permute-start.2 = (bf16[160,7168]{1,0:T(8,128)(2,1)}, bf16[160,7168]{1,0:T(8,128)(2,1)}, u32[]{:S(2)}, u32[]{:S(2)}) collective-permute-start(bf16[160,7168]{1,0:T(8,128)(2,1)} %get-tuple-element.151), channel_id=6, source_target_pairs={{0,1},{1,2},{2,3},{3,4},{4,5},{5,6},{6,7},{7,8},{8,9},{9,10},{10,1... | collective-permute-start | bytes 6881288 | tf_op jit(solution)/dot_general | solution.py:14
  1497.1 24.0 %collective-permute-start.8 = (bf16[160,7168]{1,0:T(8,128)(2,1)}, bf16[160,7168]{1,0:T(8,128)(2,1)}, u32[]{:S(2)}, u32[]{:S(2)}) collective-permute-start(bf16[160,7168]{1,0:T(8,128)(2,1)} %get-tuple-element.13), channel_id=7, source_target_pairs={{0,1},{1,2},{2,3},{3,4},{4,5},{5,6},{6,7},{7,8},{8,9},{9,10},{10,1... | collective-permute-start | bytes 6881288 | tf_op jit(solution)/dot_general | solution.py:14
  1521.1 68.7 %convolution_convert_fusion = bf16[1280,7168]{1,0:T(8,128)(2,1)} fusion(bf16[2560,7168]{1,0:T(8,128)(2,1)} %all-gather.7.cloned.1.call-done, bf16[2560,1280]{1,0:T(8,128)(2,1)} %param.6, bf16[2560,1280]{1,0:T(8,128)(2,1)} %param.7), kind=kOutput, calls=%fused_computation.48 | convolution fusion | flops 47011594240 | bytes 68157440 | tf_op jit(solution)/gta,gtb->gab/dot_general | solution.py:19
  1589.8 55.6 %fusion.32 = bf16[7168,1280]{0,1:T(8,128)(2,1)} fusion(bf16[2560,1280]{1,0:T(8,128)(2,1)} %get-tuple-element.249, bf16[2560,7168]{1,0:T(8,128)(2,1)} %all-gather.9.cloned.1.call-done), kind=kOutput, calls=%fused_computation.51 | convolution fusion | flops 46985379840 | bytes 61603840 | tf_op jit(solution)/gta,gtb->gab/dot_general | solution.py:19
  1645.4 53.4 %fusion.33 = bf16[7168,1280]{0,1:T(8,128)(2,1)} fusion(bf16[2560,1280]{1,0:T(8,128)(2,1)S(1)} %copy-done.6, bf16[2560,7168]{1,0:T(8,128)(2,1)} %all-gather.9.cloned.1.call-done), kind=kOutput, calls=%fused_computation.52 | convolution fusion | flops 46985379840 | bytes 61603840 | tf_op jit(solution)/gta,gtb->gab/dot_general | solution.py:19
  1698.8 25.0 %copy.1 = bf16[7168,1280]{1,0:T(8,128)(2,1)} copy(bf16[7168,1280]{0,1:T(8,128)(2,1)} %fusion.33) | data formatting | bytes 36700160
  1723.8 25.2 %copy = bf16[7168,1280]{1,0:T(8,128)(2,1)} copy(bf16[7168,1280]{0,1:T(8,128)(2,1)} %fusion.32) | data formatting | bytes 36700160
  (143 shorter events, 620.9 us)
Async XLA Ops:
  7.2 147.5 %all-gather.7.cloned.1.call-start = ((), (), s32[]{:S(2)}) async-start(), calls=%async_computation | async-start | bytes 38993920 | tf_op args[1]
  7.9 1581.9 %all-gather.9.cloned.1.call-start = ((), (), s32[]{:S(2)}) async-start(), calls=%async_computation.1 | async-start | bytes 38993920 | tf_op args[0]
  221.0 71.9 %collective-permute-start.5 = (bf16[160,7168]{1,0:T(8,128)(2,1)}, bf16[160,7168]{1,0:T(8,128)(2,1)}, u32[]{:S(2)}, u32[]{:S(2)}) collective-permute-start(bf16[160,7168]{1,0:T(8,128)(2,1)} %broadcast_select_fusion.11), channel_id=9, source_target_pairs={{0,15},{1,0},{2,1},{3,2},{4,3},{5,4},{6,5},{7,6},{8,7},{9,8},{10,9... | collective-permute-start | bytes 6881288 | tf_op jit(solution)/dot_general | solution.py:14
  224.7 75.9 %collective-permute-start.4 = (bf16[160,7168]{1,0:T(8,128)(2,1)}, bf16[160,7168]{1,0:T(8,128)(2,1)}, u32[]{:S(2)}, u32[]{:S(2)}) collective-permute-start(bf16[160,7168]{1,0:T(8,128)(2,1)} %broadcast_select_fusion.10), channel_id=10, source_target_pairs={{0,1},{1,2},{2,3},{3,4},{4,5},{5,6},{6,7},{7,8},{8,9},{9,10},{10,1... | collective-permute-start | bytes 6881288 | tf_op jit(solution)/dot_general | solution.py:14
  361.0 70.7 %collective-permute-start.5 = (bf16[160,7168]{1,0:T(8,128)(2,1)}, bf16[160,7168]{1,0:T(8,128)(2,1)}, u32[]{:S(2)}, u32[]{:S(2)}) collective-permute-start(bf16[160,7168]{1,0:T(8,128)(2,1)} %broadcast_select_fusion.11), channel_id=9, source_target_pairs={{0,15},{1,0},{2,1},{3,2},{4,3},{5,4},{6,5},{7,6},{8,7},{9,8},{10,9... | collective-permute-start | bytes 6881288 | tf_op jit(solution)/dot_general | solution.py:14
  366.3 86.3 %collective-permute-start.4 = (bf16[160,7168]{1,0:T(8,128)(2,1)}, bf16[160,7168]{1,0:T(8,128)(2,1)}, u32[]{:S(2)}, u32[]{:S(2)}) collective-permute-start(bf16[160,7168]{1,0:T(8,128)(2,1)} %broadcast_select_fusion.10), channel_id=10, source_target_pairs={{0,1},{1,2},{2,3},{3,4},{4,5},{5,6},{6,7},{7,8},{8,9},{9,10},{10,1... | collective-permute-start | bytes 6881288 | tf_op jit(solution)/dot_general | solution.py:14
  537.0 60.2 %collective-permute-start.5 = (bf16[160,7168]{1,0:T(8,128)(2,1)}, bf16[160,7168]{1,0:T(8,128)(2,1)}, u32[]{:S(2)}, u32[]{:S(2)}) collective-permute-start(bf16[160,7168]{1,0:T(8,128)(2,1)} %broadcast_select_fusion.11), channel_id=9, source_target_pairs={{0,15},{1,0},{2,1},{3,2},{4,3},{5,4},{6,5},{7,6},{8,7},{9,8},{10,9... | collective-permute-start | bytes 6881288 | tf_op jit(solution)/dot_general | solution.py:14
  542.3 75.7 %collective-permute-start.4 = (bf16[160,7168]{1,0:T(8,128)(2,1)}, bf16[160,7168]{1,0:T(8,128)(2,1)}, u32[]{:S(2)}, u32[]{:S(2)}) collective-permute-start(bf16[160,7168]{1,0:T(8,128)(2,1)} %broadcast_select_fusion.10), channel_id=10, source_target_pairs={{0,1},{1,2},{2,3},{3,4},{4,5},{5,6},{6,7},{7,8},{8,9},{9,10},{10,1... | collective-permute-start | bytes 6881288 | tf_op jit(solution)/dot_general | solution.py:14
  623.1 55.1 %collective-permute-start.6 = (bf16[160,7168]{1,0:T(8,128)(2,1)}, bf16[160,7168]{1,0:T(8,128)(2,1)}, u32[]{:S(2)}, u32[]{:S(2)}) collective-permute-start(bf16[160,7168]{1,0:T(8,128)(2,1)} %get-tuple-element.160), channel_id=12, source_target_pairs={{0,1},{1,2},{2,3},{3,4},{4,5},{5,6},{6,7},{7,8},{8,9},{9,10},{10,1... | collective-permute-start | bytes 6881288 | tf_op jit(solution)/dot_general | solution.py:14
  702.5 60.1 %collective-permute-start.5 = (bf16[160,7168]{1,0:T(8,128)(2,1)}, bf16[160,7168]{1,0:T(8,128)(2,1)}, u32[]{:S(2)}, u32[]{:S(2)}) collective-permute-start(bf16[160,7168]{1,0:T(8,128)(2,1)} %broadcast_select_fusion.11), channel_id=9, source_target_pairs={{0,15},{1,0},{2,1},{3,2},{4,3},{5,4},{6,5},{7,6},{8,7},{9,8},{10,9... | collective-permute-start | bytes 6881288 | tf_op jit(solution)/dot_general | solution.py:14
  707.7 75.7 %collective-permute-start.4 = (bf16[160,7168]{1,0:T(8,128)(2,1)}, bf16[160,7168]{1,0:T(8,128)(2,1)}, u32[]{:S(2)}, u32[]{:S(2)}) collective-permute-start(bf16[160,7168]{1,0:T(8,128)(2,1)} %broadcast_select_fusion.10), channel_id=10, source_target_pairs={{0,1},{1,2},{2,3},{3,4},{4,5},{5,6},{6,7},{7,8},{8,9},{9,10},{10,1... | collective-permute-start | bytes 6881288 | tf_op jit(solution)/dot_general | solution.py:14
  788.6 55.1 %collective-permute-start.6 = (bf16[160,7168]{1,0:T(8,128)(2,1)}, bf16[160,7168]{1,0:T(8,128)(2,1)}, u32[]{:S(2)}, u32[]{:S(2)}) collective-permute-start(bf16[160,7168]{1,0:T(8,128)(2,1)} %get-tuple-element.160), channel_id=12, source_target_pairs={{0,1},{1,2},{2,3},{3,4},{4,5},{5,6},{6,7},{7,8},{8,9},{9,10},{10,1... | collective-permute-start | bytes 6881288 | tf_op jit(solution)/dot_general | solution.py:14
  864.6 884.4 %collective-permute-start.9 = (bf16[160,7168]{1,0:T(8,128)(2,1)}, bf16[160,7168]{1,0:T(8,128)(2,1)}, u32[]{:S(2)}, u32[]{:S(2)}) collective-permute-start(bf16[160,7168]{1,0:T(8,128)(2,1)} %get-tuple-element.15), channel_id=13, source_target_pairs={{0,1},{1,2},{2,3},{3,4},{4,5},{5,6},{6,7},{7,8},{8,9},{9,10},{10,1... | collective-permute-start | bytes 6881288 | tf_op jit(solution)/dot_general | solution.py:14
  927.1 58.5 %collective-permute-start.2 = (bf16[160,7168]{1,0:T(8,128)(2,1)}, bf16[160,7168]{1,0:T(8,128)(2,1)}, u32[]{:S(2)}, u32[]{:S(2)}) collective-permute-start(bf16[160,7168]{1,0:T(8,128)(2,1)} %get-tuple-element.151), channel_id=6, source_target_pairs={{0,1},{1,2},{2,3},{3,4},{4,5},{5,6},{6,7},{7,8},{8,9},{9,10},{10,1... | collective-permute-start | bytes 6881288 | tf_op jit(solution)/dot_general | solution.py:14
  1007.2 61.0 %collective-permute-start.1 = (bf16[160,7168]{1,0:T(8,128)(2,1)}, bf16[160,7168]{1,0:T(8,128)(2,1)S(1)}, u32[]{:S(2)}, u32[]{:S(2)}) collective-permute-start(bf16[160,7168]{1,0:T(8,128)(2,1)} %broadcast_select_fusion.9), channel_id=3, source_target_pairs={{0,15},{1,0},{2,1},{3,2},{4,3},{5,4},{6,5},{7,6},{8,7},{9,8},{10,9... | collective-permute-start | bytes 6881288 | tf_op jit(solution)/dot_general | solution.py:14
  1012.5 75.7 %collective-permute-start = (bf16[160,7168]{1,0:T(8,128)(2,1)}, bf16[160,7168]{1,0:T(8,128)(2,1)}, u32[]{:S(2)}, u32[]{:S(2)}) collective-permute-start(bf16[160,7168]{1,0:T(8,128)(2,1)} %broadcast_select_fusion.8), channel_id=4, source_target_pairs={{0,1},{1,2},{2,3},{3,4},{4,5},{5,6},{6,7},{7,8},{8,9},{9,10},{10,1... | collective-permute-start | bytes 6881288 | tf_op jit(solution)/dot_general | solution.py:14
  1092.6 56.8 %collective-permute-start.2 = (bf16[160,7168]{1,0:T(8,128)(2,1)}, bf16[160,7168]{1,0:T(8,128)(2,1)}, u32[]{:S(2)}, u32[]{:S(2)}) collective-permute-start(bf16[160,7168]{1,0:T(8,128)(2,1)} %get-tuple-element.151), channel_id=6, source_target_pairs={{0,1},{1,2},{2,3},{3,4},{4,5},{5,6},{6,7},{7,8},{8,9},{9,10},{10,1... | collective-permute-start | bytes 6881288 | tf_op jit(solution)/dot_general | solution.py:14
  1171.0 61.0 %collective-permute-start.1 = (bf16[160,7168]{1,0:T(8,128)(2,1)}, bf16[160,7168]{1,0:T(8,128)(2,1)S(1)}, u32[]{:S(2)}, u32[]{:S(2)}) collective-permute-start(bf16[160,7168]{1,0:T(8,128)(2,1)} %broadcast_select_fusion.9), channel_id=3, source_target_pairs={{0,15},{1,0},{2,1},{3,2},{4,3},{5,4},{6,5},{7,6},{8,7},{9,8},{10,9... | collective-permute-start | bytes 6881288 | tf_op jit(solution)/dot_general | solution.py:14
  1176.3 75.7 %collective-permute-start = (bf16[160,7168]{1,0:T(8,128)(2,1)}, bf16[160,7168]{1,0:T(8,128)(2,1)}, u32[]{:S(2)}, u32[]{:S(2)}) collective-permute-start(bf16[160,7168]{1,0:T(8,128)(2,1)} %broadcast_select_fusion.8), channel_id=4, source_target_pairs={{0,1},{1,2},{2,3},{3,4},{4,5},{5,6},{6,7},{7,8},{8,9},{9,10},{10,1... | collective-permute-start | bytes 6881288 | tf_op jit(solution)/dot_general | solution.py:14
  1256.4 56.8 %collective-permute-start.2 = (bf16[160,7168]{1,0:T(8,128)(2,1)}, bf16[160,7168]{1,0:T(8,128)(2,1)}, u32[]{:S(2)}, u32[]{:S(2)}) collective-permute-start(bf16[160,7168]{1,0:T(8,128)(2,1)} %get-tuple-element.151), channel_id=6, source_target_pairs={{0,1},{1,2},{2,3},{3,4},{4,5},{5,6},{6,7},{7,8},{8,9},{9,10},{10,1... | collective-permute-start | bytes 6881288 | tf_op jit(solution)/dot_general | solution.py:14
  1334.8 61.0 %collective-permute-start.1 = (bf16[160,7168]{1,0:T(8,128)(2,1)}, bf16[160,7168]{1,0:T(8,128)(2,1)S(1)}, u32[]{:S(2)}, u32[]{:S(2)}) collective-permute-start(bf16[160,7168]{1,0:T(8,128)(2,1)} %broadcast_select_fusion.9), channel_id=3, source_target_pairs={{0,15},{1,0},{2,1},{3,2},{4,3},{5,4},{6,5},{7,6},{8,7},{9,8},{10,9... | collective-permute-start | bytes 6881288 | tf_op jit(solution)/dot_general | solution.py:14
  1340.1 75.7 %collective-permute-start = (bf16[160,7168]{1,0:T(8,128)(2,1)}, bf16[160,7168]{1,0:T(8,128)(2,1)}, u32[]{:S(2)}, u32[]{:S(2)}) collective-permute-start(bf16[160,7168]{1,0:T(8,128)(2,1)} %broadcast_select_fusion.8), channel_id=4, source_target_pairs={{0,1},{1,2},{2,3},{3,4},{4,5},{5,6},{6,7},{7,8},{8,9},{9,10},{10,1... | collective-permute-start | bytes 6881288 | tf_op jit(solution)/dot_general | solution.py:14
  1420.2 56.8 %collective-permute-start.2 = (bf16[160,7168]{1,0:T(8,128)(2,1)}, bf16[160,7168]{1,0:T(8,128)(2,1)}, u32[]{:S(2)}, u32[]{:S(2)}) collective-permute-start(bf16[160,7168]{1,0:T(8,128)(2,1)} %get-tuple-element.151), channel_id=6, source_target_pairs={{0,1},{1,2},{2,3},{3,4},{4,5},{5,6},{6,7},{7,8},{8,9},{9,10},{10,1... | collective-permute-start | bytes 6881288 | tf_op jit(solution)/dot_general | solution.py:14
  1497.1 251.9 %collective-permute-start.8 = (bf16[160,7168]{1,0:T(8,128)(2,1)}, bf16[160,7168]{1,0:T(8,128)(2,1)}, u32[]{:S(2)}, u32[]{:S(2)}) collective-permute-start(bf16[160,7168]{1,0:T(8,128)(2,1)} %get-tuple-element.13), channel_id=7, source_target_pairs={{0,1},{1,2},{2,3},{3,4},{4,5},{5,6},{6,7},{7,8},{8,9},{9,10},{10,1... | collective-permute-start | bytes 6881288 | tf_op jit(solution)/dot_general | solution.py:14
  (28 other events, 1248.4 us)
Sparse Core Ops, SparseCore 0:
  10.2 144.3 all-gather.6
  156.9 220.4 all-gather.8
where the time goes:
time: 1770 us; the launch traced here: 1760 us
  starting transfers between devices  700 us (40%)
  waiting for transfers between devices  472 us (27%)
  matrix products  404 us (23%)
  other arithmetic  113 us (6%)
  local copies, waits for them, and re-layouts  57.2 us (3%)
    dot_general x34, starting transfers between devices, step(): dx = jnp.dot(d_gate, w_gate.T) + jnp.dot(d_up, w_up.T)  700 us
    dot_general x34, waiting for transfers between devices, step(): dx = jnp.dot(d_gate, w_gate.T) + jnp.dot(d_up, w_up.T)  324 us
    dot_general x3, matrix products, by_group(): jnp.einsum('gta,gtb->gab', a, b, preferred_element_type=jnp.float32)  178 us
    dot_general x16, matrix products, step(): dx = jnp.dot(d_gate, w_gate.T) + jnp.dot(d_up, w_up.T)  162 us
    unnamed x4, waiting for transfers between devices  147 us
    dot_general x16, other arithmetic, step(): dx = jnp.dot(d_gate, w_gate.T) + jnp.dot(d_up, w_up.T)  76.9 us
    dot_general x1, matrix products, step(): d_hidden = jnp.dot(dy, w_down.T, preferred_element_type=jnp.float32)  64.6 us
    unnamed x10, local copies, waits for them, and re-layouts  50.2 us
  transfers between devices with their start and end apart: 36, of which 20 were waited for; matrix products, arithmetic and copies ran while one was open for 32% of the time, Pallas kernels for 0%

commit v1 on v0

v1 whole, which is shorter than its diff:
```python
import functools
import jax
import jax.numpy as jnp
from jax import lax
from jax.experimental import pallas as pl
from jax.experimental.pallas import tpu as pltpu
from jax.sharding import PartitionSpec as P

F32, BF16 = jnp.float32, jnp.bfloat16
NT = (((1,), (1,)), ((), ()))
TN = (((0,), (0,)), ((), ()))
L1, L2, L3 = 3, 2, 2
LAG = 1 + L1 + L2 + L3
OWN, SIB, SND = LAG + 1, LAG + 2, 3


def weight(j):
    return (8 - 5 * j + j * j) // 2


def flip(i, w):
    return i + w - 2 * w * ((i // w) % 2)


def rs_kernel(tiles, dg_hbm, du_hbm, wg_hbm, wu_hbm, dx_ref, dg, w, own, sib, s0, s1, r1, s2, r2, s3, r3,
              dg_sem, w_sem, s0_sem, sib_sem, s1_sem, r1_sem, s2_sem, r2_sem, s3_sem, r3_sem, free_sem):
    me = lax.axis_index("tp")
    chip, core = me // 2, me % 2
    rows, k = dg.shape[2], dg_hbm.shape[1]
    ct = w.shape[1]

    def dev(i):
        return {"tp": i}

    barrier = pltpu.get_barrier_semaphore()
    for m in (1, 2, 4, 8):
        pl.semaphore_signal(barrier, inc=1, device_id=dev(flip(me, m)), device_id_type=pl.DeviceIdType.MESH)

    def load_block(c, r, half, src):
        other = (core + 1 - c) % 2
        target = chip
        for wt in (4, 2, 1):
            if r & wt:
                target = flip(target, wt)
        return pltpu.make_async_copy(
            src.at[pl.ds((target * 2 + other) * rows, rows)],
            dg.at[c, r, :, pl.ds(half * k, k)],
            dg_sem.at[(c * 8 + r) * 2 + half],
        )

    blocks = [load_block(c, r, h, s) for c in range(2) for r in range(8) for h, s in ((0, dg_hbm), (1, du_hbm))]

    def load_w(t, slot):
        return [
            pltpu.make_async_copy(s.at[pl.ds(t * ct, ct)], w.at[slot, :, pl.ds(h * k, k)], w_sem.at[slot, h])
            for h, s in ((0, wg_hbm), (1, wu_hbm))
        ]

    for c in load_w(0, 0):
        c.start()
    for b in blocks:
        b.start()
    for b in blocks:
        b.wait()
    pl.semaphore_wait(barrier, 4)

    def remote(src, dst, ssem, rsem, to):
        return pltpu.make_async_remote_copy(
            src_ref=src, dst_ref=dst, send_sem=ssem, recv_sem=rsem, device_id=dev(to),
            device_id_type=pl.DeviceIdType.MESH)

    def c0(t):
        return remote(s0.at[t % SND], sib.at[t % SIB], s0_sem.at[t % SND], sib_sem.at[t % SIB], flip(me, 1))

    def axes(t):
        j = t % 3
        return weight(j), weight((j + 1) % 3), weight((j + 2) % 3)

    def c1(t):
        return remote(s1.at[t % SND], r1.at[t], s1_sem.at[t % SND], r1_sem.at[t], flip(me, 2 * axes(t)[0]))

    def c2(t):
        return remote(s2.at[t % SND], r2.at[t], s2_sem.at[t % SND], r2_sem.at[t], flip(me, 2 * axes(t)[1]))

    def c3(t):
        return remote(s3.at[t % SND], r3.at[t], s3_sem.at[t % SND], r3_sem.at[t], flip(me, 2 * axes(t)[2]))

    def base(t, r):
        return own[t % OWN, r] + sib[t % SIB, r].astype(F32)

    def when(cond, f):
        pl.when(cond)(f)

    def step(i, _):
        slot = i % 2

        @pl.when(i < tiles)
        def _():
            @pl.when(i + 1 < tiles)
            def _():
                for c in load_w(i + 1, (i + 1) % 2):
                    c.start()
            for c in load_w(i, slot):
                c.wait()
            @pl.when(i >= SND)
            def _():
                c0(i - SND).wait_send()
            part = lax.dot_general(dg[0].reshape(8 * rows, 2 * k), w[slot], NT, preferred_element_type=F32)
            s0[i % SND] = part.astype(BF16).reshape(8, rows, ct)

        t = i - 1

        @pl.when((t >= 0) & (t < tiles))
        def _():
            @pl.when(t >= SND)
            def _():
                c1(t - SND).wait_send()
            c0(t).wait_recv()
            a, b, c = axes(t)
            for q, r in enumerate((a, a + c, a + b, a + b + c)):
                s1[t % SND, q] = base(t, r).astype(BF16)

        t2 = i - 1 - L1

        @pl.when((t2 >= 0) & (t2 < tiles))
        def _():
            @pl.when(t2 >= SND)
            def _():
                c2(t2 - SND).wait_send()
            c1(t2).wait_recv()
            a, b, c = axes(t2)
            for q, r in enumerate((b, b + c)):
                s2[t2 % SND, q] = (base(t2, r) + r1[t2, 2 + q].astype(F32)).astype(BF16)

        t3 = i - 1 - L1 - L2

        @pl.when((t3 >= 0) & (t3 < tiles))
        def _():
            @pl.when(t3 >= SND)
            def _():
                c3(t3 - SND).wait_send()
            c2(t3).wait_recv()
            a, b, c = axes(t3)
            s3[t3 % SND] = (base(t3, c) + r1[t3, 1].astype(F32) + r2[t3, 1].astype(F32)).astype(BF16)

        t4 = i - LAG

        @pl.when((t4 >= 0) & (t4 < tiles))
        def _():
            c3(t4).wait_recv()
            total = base(t4, 0) + r1[t4, 0].astype(F32) + r2[t4, 0].astype(F32) + r3[t4].astype(F32)
            dx_ref[:, pl.ds(pl.multiple_of(t4 * ct, ct), ct)] = total.astype(BF16)

            @pl.when(t4 < tiles - SIB)
            def _():
                pl.semaphore_signal(free_sem, inc=1, device_id=dev(flip(me, 1)), device_id_type=pl.DeviceIdType.MESH)

        @pl.when(i < tiles)
        def _():
            @pl.when(i >= SIB)
            def _():
                pl.semaphore_wait(free_sem, 1)
            c0(i).start()

        @pl.when((t >= 0) & (t < tiles))
        def _():
            c1(t).start()

        @pl.when((t2 >= 0) & (t2 < tiles))
        def _():
            c2(t2).start()

        @pl.when((t3 >= 0) & (t3 < tiles))
        def _():
            c3(t3).start()

        @pl.when(i < tiles)
        def _():
            part = lax.dot_general(dg[1].reshape(8 * rows, 2 * k), w[slot], NT, preferred_element_type=F32)
            own[i % OWN] = part.reshape(8, rows, ct)
        return 0

    lax.fori_loop(0, tiles + LAG, step, 0)
    for t in range(tiles - SND, tiles):
        for c in (c0, c1, c2, c3):
            c(t).wait_send()


def dx_reduce_scatter(d_gate, d_up, w_gate, w_up, ct=256):
    n, k = d_gate.shape
    d = w_gate.shape[0]
    rows, tiles = n // 16, d // ct
    any_ = pl.BlockSpec(memory_space=pl.ANY)
    dma = pltpu.SemaphoreType.DMA
    v = pltpu.VMEM
    return pl.pallas_call(
        functools.partial(rs_kernel, tiles),
        out_shape=jax.ShapeDtypeStruct((rows, d), BF16),
        in_specs=[any_] * 4,
        out_specs=pl.BlockSpec(memory_space=pltpu.VMEM),
        scratch_shapes=[
            v((2, 8, rows, 2 * k), BF16), v((2, ct, 2 * k), BF16), v((OWN, 8, rows, ct), F32),
            v((SIB, 8, rows, ct), BF16), v((SND, 8, rows, ct), BF16),
            v((SND, 4, rows, ct), BF16), v((tiles, 4, rows, ct), BF16),
            v((SND, 2, rows, ct), BF16), v((tiles, 2, rows, ct), BF16),
            v((SND, rows, ct), BF16), v((tiles, rows, ct), BF16),
            dma((32,)), dma((2, 2)), dma((SND,)), dma((SIB,)), dma((SND,)), dma((tiles,)),
            dma((SND,)), dma((tiles,)), dma((SND,)), dma((tiles,)), pltpu.SemaphoreType.REGULAR,
        ],
        compiler_params=pltpu.CompilerParams(collective_id=0, has_side_effects=True, vmem_limit_bytes=66000000),
        cost_estimate=pl.CostEstimate(flops=2 * n * k * d * 2, bytes_accessed=4 * n * k + 4 * k * d, transcendentals=0),
    )(d_gate, d_up, w_gate, w_up)


def act(gate, up):
    return jax.nn.silu(gate) * up


def solution(mesh):
    def body(x, dy, gate, up, w_gate, w_up, w_down):
        dy_all = lax.all_gather(dy, "tp", tiled=True)
        hidden, back = jax.vjp(act, gate.astype(F32), up.astype(F32))
        d_hidden = lax.dot_general(dy_all, w_down, NT, preferred_element_type=F32)
        d_gate, d_up = (g.astype(BF16) for g in back(d_hidden))
        dx = dx_reduce_scatter(d_gate, d_up, w_gate, w_up)
        x_all = lax.all_gather(x, "tp", tiled=True)
        dw_gate = lax.dot_general(x_all, d_gate, TN, preferred_element_type=F32).astype(BF16)
        dw_up = lax.dot_general(x_all, d_up, TN, preferred_element_type=F32).astype(BF16)
        dw_down = lax.dot_general(hidden.astype(BF16), dy_all, TN, preferred_element_type=F32).astype(BF16)
        return dx, dw_gate, dw_up, dw_down

    rows, cols = P(("dp", "tp"), None), P("dp", "tp")
    return jax.shard_map(
        body,
        mesh=mesh,
        in_specs=(rows, rows, cols, cols, P(None, "tp"), P(None, "tp"), P("tp", None)),
        out_specs=(rows, cols, cols, P(("dp", "tp"), None)),
        check_vma=False,
    )
```

time: 1770 us -> 666 us (0.38)
  starting transfers between devices: 700 us -> 0.08 us
  waiting for transfers between devices: 472 us -> 147 us
  Pallas kernels: 0 us -> 208 us
  matrix products: 404 us -> 244 us
  other arithmetic: 113 us -> 0 us
    dot_general x34 -> x0, starting transfers between devices: 700 us -> none  [step(): dx = jnp.dot(d_gate, w_gate.T) + jnp.dot(d_up, w_up.T)]
    dot_general x34 -> x0, waiting for transfers between devices: 324 us -> none  [step(): dx = jnp.dot(d_gate, w_gate.T) + jnp.dot(d_up, w_up.T)]
    pallas_call x0 -> x1, Pallas kernels: none -> 208 us  [dx_reduce_scatter(): pl.pallas_call(functools.partial(rs_kernel, tiles), out_shape=jax.ShapeDt...]
    dot_general x20 -> x4, matrix products: 404 us -> 244 us  [the longest x1 68.9 us: body(): lax.dot_general(hidden.astype(BF16), dy_all, TN, preferred_element_type=F32)]
    all_gather x0 -> x2, waiting for transfers between devices: none -> 146 us  [the longest x1 146 us: body(): dy_all = lax.all_gather(dy, 'tp', tiled=True)]
    unnamed x4 -> x2, waiting for transfers between devices: 147 us -> 1.38 us
    dot_general x32 -> x0, other arithmetic: 108 us -> none  [the longest x16 76.9 us: step(): dx = jnp.dot(d_gate, w_gate.T) + jnp.dot(d_up, w_up.T)]
    unnamed x10 -> x5, local copies, waits for them, and re-layouts: 50.2 us -> 51.4 us
  transfers between devices with their start and end apart: 36 -> 2, of which waited for: 20 -> 1; matrix products, arithmetic and copies ran while one was open for 32% -> 10% of each run, Pallas kernels for 0% -> 31%
where the time goes in v1:
time: 666 us; the launch traced here: 665 us
  matrix products  244 us (37%)
  Pallas kernels  208 us (31%)
  waiting for transfers between devices  147 us (22%)
  local copies, waits for them, and re-layouts  51.4 us (8%)
  between operations  14.1 us (2%)
    pallas_call x1, Pallas kernels, dx_reduce_scatter(): pl.pallas_call(functools.partial(rs_kernel, tiles), out_shape=jax.ShapeDt...  208 us
    all_gather x1, waiting for transfers between devices, body(): dy_all = lax.all_gather(dy, 'tp', tiled=True)  146 us
    dot_general x1, matrix products, body(): lax.dot_general(hidden.astype(BF16), dy_all, TN, preferred_element_type=F32)  68.9 us
    dot_general x1, matrix products, body(): d_hidden = lax.dot_general(dy_all, w_down, NT, preferred_element_type=F32)  64.6 us
    dot_general x1, matrix products, body(): lax.dot_general(x_all, d_gate, TN, preferred_element_type=F32).astype(BF16)  55.3 us
    dot_general x1, matrix products, body(): lax.dot_general(x_all, d_up, TN, preferred_element_type=F32).astype(BF16)  55.1 us
    unnamed x5, local copies, waits for them, and re-layouts  51.4 us
  transfers between devices with their start and end apart: 2, of which 1 were waited for; matrix products, arithmetic and copies ran while one was open for 10% of the time, Pallas kernels for 31%

profile of v1, /device:TPU:0, one launch (start us, length us, event | category | flops | bytes accessed | tf_op | source)
XLA Modules:
  0.0 665.0 jit_solution(11422046483261893045)
XLA Ops:
  7.2 0.0 all-gather.3.cloned.1.call-start
  7.2 0.7 all-gather.3.cloned.1.call-update
  7.9 0.0 all-gather.5.cloned.1.call-start
  7.9 0.7 all-gather.5.cloned.1.call-update
  8.6 146.0 %all-gather.3.cloned.1.call-done = bf16[2560,7168]{1,0:T(8,128)(2,1)} async-done(((bf16[160,7168]{1,0:T(8,128)(2,1)}), bf16[2560,7168]{1,0:T(8,128)(2,1)}) %all-gather.3.cloned.1.call-update) | async-done | bytes 36700176 | tf_op jit(solution)/shard_map/all_gather | solution.py:221
  154.6 64.6 %multiply_convert_fusion = (bf16[2560,1280]{1,0:T(8,128)(2,1)}, bf16[2560,1280]{1,0:T(8,128)(2,1)}) fusion(bf16[2560,1280]{1,0:T(8,128)(2,1)} %param.9, bf16[2560,1280]{1,0:T(8,128)(2,1)} %param.10, bf16[2560,7168]{1,0:T(8,128)(2,1)} %all-gather.3.cloned.1.call-done, bf16[1280,7168]{1,0:T(8,128)(2,1)} %param.13), kind=kOutput, calls=%fused_computation.18 | convolution fusion | flops 47028633600 | bytes 81264640 | tf_op jit(solution)/shard_map/dot_general | solution.py:223
  219.2 208.2 %shard_map.102 = bf16[160,7168]{1,0:T(8,128)(2,1)} custom-call(bf16[2560,1280]{1,0:T(8,128)(2,1)} %get-tuple-element.9.dg_hbm, bf16[2560,1280]{1,0:T(8,128)(2,1)} %get-tuple-element.8.du_hbm, bf16[7168,1280]{1,0:T(8,128)(2,1)} %wg_hbm.1, bf16[7168,1280]{1,0:T(8,128)(2,1)} %wu_hbm.1), custom_call_target="tpu_custom_call" | custom-call | flops 93952409600 | bytes 49807360 | tf_op jit(solution)/shard_map/pallas_call | solution.py:196
  427.4 0.0 all-gather.5.cloned.1.call-done
  427.4 55.3 %fusion = bf16[7168,1280]{0,1:T(8,128)(2,1)} fusion(bf16[2560,1280]{1,0:T(8,128)(2,1)} %get-tuple-element.9.dg_hbm, bf16[2560,7168]{1,0:T(8,128)(2,1)} %all-gather.5.cloned.1.call-done), kind=kOutput, calls=%fused_computation.3 | convolution fusion | flops 46985379840 | bytes 61603840 | tf_op jit(solution)/shard_map/dot_general | solution.py:227
  482.7 25.0 %copy.11 = bf16[7168,1280]{1,0:T(8,128)(2,1)} copy(bf16[7168,1280]{0,1:T(8,128)(2,1)} %fusion) | data formatting | bytes 36700160
  507.7 55.1 %fusion.1 = bf16[7168,1280]{0,1:T(8,128)(2,1)} fusion(bf16[2560,1280]{1,0:T(8,128)(2,1)} %get-tuple-element.8.du_hbm, bf16[2560,7168]{1,0:T(8,128)(2,1)} %all-gather.5.cloned.1.call-done), kind=kOutput, calls=%fused_computation.4 | convolution fusion | flops 46985379840 | bytes 61603840 | tf_op jit(solution)/shard_map/dot_general | solution.py:228
  562.9 25.0 %copy.12 = bf16[7168,1280]{1,0:T(8,128)(2,1)} copy(bf16[7168,1280]{0,1:T(8,128)(2,1)} %fusion.1) | data formatting | bytes 36700160
  587.9 0.0 copy-start
  587.9 68.9 %convolution_convert_fusion = bf16[1280,7168]{1,0:T(8,128)(2,1)} fusion(bf16[2560,7168]{1,0:T(8,128)(2,1)} %all-gather.3.cloned.1.call-done, bf16[2560,1280]{1,0:T(8,128)(2,1)} %param.10, bf16[2560,1280]{1,0:T(8,128)(2,1)} %param.9), kind=kOutput, calls=%fused_computation | convolution fusion | flops 47011594240 | bytes 68157440 | tf_op jit(solution)/shard_map/dot_general | solution.py:229
  656.7 0.0 copy-done
  656.7 1.4 copy.14
Async XLA Ops:
  7.2 147.5 %all-gather.3.cloned.1.call-start = ((), (), s32[]{:S(2)}) async-start(), calls=%async_computation | async-start | bytes 38993920 | tf_op jit(solution)/shard_map/all_gather | solution.py:221
  7.9 419.5 %all-gather.5.cloned.1.call-start = ((), (), s32[]{:S(2)}) async-start(), calls=%async_computation.1 | async-start | bytes 38993920 | tf_op jit(solution)/shard_map/all_gather | solution.py:226
  587.9 68.9 %copy-start = (bf16[160,7168]{1,0:T(8,128)(2,1)S(1)}, bf16[160,7168]{1,0:T(8,128)(2,1)}, u32[]{:S(2)}) copy-start(bf16[160,7168]{1,0:T(8,128)(2,1)} %shard_map.102) | copy-start | bytes 6881284
Sparse Core Ops, SparseCore 0:
  10.2 144.3 all-gather.2
  156.9 191.6 all-gather.4

commit v2 on v0

v2 whole, which is shorter than its diff:
```python
import functools

import jax
import jax.numpy as jnp
from jax import lax
from jax.experimental import pallas as pl
from jax.experimental.pallas import tpu as pltpu
from jax.sharding import PartitionSpec as P

F32, BF16 = jnp.float32, jnp.bfloat16
NT = (((1,), (1,)), ((), ()))
TN = (((0,), (0,)), ((), ()))
MESH = pl.DeviceIdType.MESH

A1, A2, A3 = 2, 2, 3
LAG_A = A1 + A2 + A3 + 1
B1, B2, B3 = 3, 2, 2
LAG_B = 1 + B1 + B2 + B3
NS = 10
NR = 10
SND = 3


def weight(j):
    return (8 - 5 * j + j * j) // 2


def flip(i, w):
    return i + w - 2 * w * ((i // w) % 2)


def axes(t):
    j = t % 3
    return weight(j), weight((j + 1) % 3), weight((j + 2) % 3)


def remote(src, dst, ssem, rsem, to):
    return pltpu.make_async_remote_copy(
        src_ref=src, dst_ref=dst, send_sem=ssem, recv_sem=rsem, device_id={"tp": to}, device_id_type=MESH
    )


def kernel(
    tiles, x_hbm, dy_hbm, gate_hbm, up_hbm, wg_hbm, wu_hbm, wd_hbm, dx_ref, dwg_hbm, dwu_hbm, dwd_hbm,
    ag, acc, hid, dg, w, wd, dwd, s0, s1, s2, s3, r1, r2, r3,
    ag_send, ag_recv, own_sem, load_sem, w_sem, wd_sem, dwd_sem, out_sem,
    s0_sem, s1_sem, s2_sem, s3_sem, r0_sem, r1_sem, r2_sem, r3_sem, credit_a, credit_b,
):
    me = lax.axis_index("tp")
    chip, core = me // 2, me % 2
    rows, ct = s3.shape[1], s3.shape[2]
    ff = gate_hbm.shape[1]
    nf = ff // ct
    half = 8 * rows
    peers = [flip(me, m) for m in (1, 2, 4, 8)]

    barrier = pltpu.get_barrier_semaphore()
    for p in peers:
        pl.semaphore_signal(barrier, inc=1, device_id={"tp": p}, device_id_type=MESH)

    def give(sem, n=1):
        for m, p in enumerate(peers):
            pl.semaphore_signal(sem.at[m], inc=n, device_id={"tp": p}, device_id_type=MESH)

    def take(sem):
        for m in range(4):
            pl.semaphore_wait(sem.at[m], 1)

    def load_rows(b, h):
        c, r = b // 8, b % 8
        target = chip
        for wt in (4, 2, 1):
            target = target + wt * ((r // wt) % 2) * (1 - 2 * ((chip // wt) % 2))
        src = (gate_hbm, up_hbm)[h]
        return pltpu.make_async_copy(
            src.at[pl.ds((target * 2 + (core + 1 - c) % 2) * rows, rows)],
            dg.at[c, r, :, pl.ds(h * ff, ff)],
            load_sem.at[b, h],
        )

    def cols(t):
        return pl.ds(pl.multiple_of(t * ct, ct), ct)

    def own_load(src, t, slot):
        return pltpu.make_async_copy(src.at[:, cols(t)], ag.at[slot, 1, 0], own_sem.at[slot])

    def hop(slot, q, m):
        return remote(
            ag.at[slot, 1, q], ag.at[slot, 1, q + m], ag_send.at[slot, q + m], ag_recv.at[slot, q + m], flip(me, 2 * m)
        )

    def share(slot):
        return remote(ag.at[slot, 1], ag.at[slot, 0], ag_send.at[slot, 0], ag_recv.at[slot, 0], flip(me, 1))

    def gather_step(src, first, i):
        @pl.when((i >= 0) & (i < tiles))
        def _():
            g = i + first
            slot = g % NS
            own_load(src, i, slot).wait()

            @pl.when(g >= NS)
            def _():
                take(credit_a)

            hop(slot, 0, axes(g)[0]).start()

            @pl.when(i + 1 < tiles)
            def _():
                own_load(src, i + 1, (g + 1) % NS).start()

        t2 = i - A1

        @pl.when((t2 >= 0) & (t2 < tiles))
        def _():
            g = t2 + first
            slot = g % NS
            a, b, c = axes(g)
            hop(slot, 0, a).wait_recv()
            hop(slot, 0, b).start()
            hop(slot, a, b).start()

        t3 = i - A1 - A2

        @pl.when((t3 >= 0) & (t3 < tiles))
        def _():
            g = t3 + first
            slot = g % NS
            a, b, c = axes(g)
            hop(slot, 0, b).wait_recv()
            hop(slot, a, b).wait_recv()
            for q in (0, a, b, a + b):
                hop(slot, q, c).start()

        t4 = i - A1 - A2 - A3

        @pl.when((t4 >= 0) & (t4 < tiles))
        def _():
            g = t4 + first
            slot = g % NS
            a, b, c = axes(g)
            for q in (0, a, b, a + b):
                hop(slot, q, c).wait_recv()
            share(slot).start()

    def release(g, last):
        slot = g % NS
        a, b, c = axes(g)
        hop(slot, 0, a).wait_send()
        for q in (0, a):
            hop(slot, q, b).wait_send()
        for q in (0, a, b, a + b):
            hop(slot, q, c).wait_send()
        share(slot).wait_send()

        @pl.when(g < last)
        def _():
            give(credit_a)

    def load_wd(t):
        return pltpu.make_async_copy(wd_hbm.at[:, cols(t)], wd.at[t % 2], wd_sem.at[t % 2])

    def load_w(t):
        return [
            pltpu.make_async_copy(
                s.at[pl.ds(pl.multiple_of(t * ct, ct), ct)], w.at[t % 2, :, pl.ds(h * ff, ff)], w_sem.at[t % 2, h]
            )
            for h, s in ((0, wg_hbm), (1, wu_hbm))
        ]

    def store_dwd(t):
        return pltpu.make_async_copy(dwd.at[t % 2], dwd_hbm.at[:, cols(t)], dwd_sem.at[t % 2])

    own_load(dy_hbm, 0, 0).start()

    def start_rows(b, _):
        load_rows(b, 0).start()
        load_rows(b, 1).start()
        return 0

    lax.fori_loop(0, 16, start_rows, 0)
    load_wd(0).start()
    pl.semaphore_wait(barrier, 4)

    def hidden_block(b):
        c, r = b // 8, b % 8
        load_rows(b, 0).wait()
        load_rows(b, 1).wait()
        for n in range(nf):
            g = dg[c, r, :, n * ct : (n + 1) * ct].astype(F32)
            u = dg[c, r, :, ff + n * ct : ff + (n + 1) * ct].astype(F32)
            hid[pl.ds(pl.multiple_of(b * rows, rows), rows), n * ct : (n + 1) * ct] = (g * jax.nn.sigmoid(g) * u).astype(BF16)
            acc[c, r, :, n * ct : (n + 1) * ct] = jnp.zeros((rows, ct), F32)

    def fill(i, _):
        gather_step(dy_hbm, 0, i)
        per = 16 // LAG_A
        for e in range(per):
            hidden_block(i * per + e)
        return 0

    lax.fori_loop(0, LAG_A, fill, 0)

    def step_a(t, _):
        gather_step(dy_hbm, 0, t + LAG_A)
        slot = t % NS

        @pl.when(t + 1 < tiles)
        def _():
            load_wd(t + 1).start()

        load_wd(t).wait()
        share(slot).wait_recv()
        for c in range(2):
            block = ag[slot, c].reshape(half, ct)
            for n in range(nf):
                part = lax.dot_general(
                    block, wd[t % 2, n * ct : (n + 1) * ct, :], NT, preferred_element_type=F32
                )
                acc[c, :, :, n * ct : (n + 1) * ct] += part.reshape(8, rows, ct)

        @pl.when(t >= 2)
        def _():
            store_dwd(t - 2).wait()

        for n in range(nf):
            dwd[t % 2, n * ct : (n + 1) * ct, :] = lax.dot_general(
                hid[:, n * ct : (n + 1) * ct], ag[slot].reshape(2 * half, ct), TN, preferred_element_type=F32
            ).astype(BF16)
        release(t, 2 * tiles - NS)
        store_dwd(t).start()
        return 0

    lax.fori_loop(0, tiles, step_a, 0)

    give(credit_b, NR)
    for c in load_w(0):
        c.start()
    own_load(x_hbm, 0, tiles % NS).start()

    def d_act(b, _):
        @pl.when(b % 4 == 0)
        def _():
            gather_step(x_hbm, tiles, b // 4)

        c, r = b // 8, b % 8
        for n in range(nf):
            lo, hi = slice(n * ct, (n + 1) * ct), slice(ff + n * ct, ff + (n + 1) * ct)
            g, u, d = dg[c, r, :, lo].astype(F32), dg[c, r, :, hi].astype(F32), acc[c, r, :, lo]
            s = jax.nn.sigmoid(g)
            dg[c, r, :, lo] = (d * u * (s + g * s * (1.0 - s))).astype(BF16)
            dg[c, r, :, hi] = (d * (g * s)).astype(BF16)
        return 0

    lax.fori_loop(0, 16, d_act, 0)
    for t in (tiles - 2, tiles - 1):
        store_dwd(t).wait()

    def place(t):
        k = t % NR
        return k // nf, pl.ds(pl.multiple_of((k % nf) * ct, ct), ct)

    def c0(t):
        c, n = place(t)
        return remote(s0.at[t % SND], hid.at[pl.ds(pl.multiple_of(c * half, half), half), n], s0_sem.at[t % SND], r0_sem.at[t % NR], flip(me, 1))

    def c1(t):
        return remote(
            s1.at[t % SND], r1.at[t % NR], s1_sem.at[t % SND], r1_sem.at[t % NR], flip(me, 2 * axes(t)[0])
        )

    def c2(t):
        return remote(
            s2.at[t % SND], r2.at[t % NR], s2_sem.at[t % SND], r2_sem.at[t % NR], flip(me, 2 * axes(t)[1])
        )

    def c3(t):
        return remote(
            s3.at[t % SND], r3.at[t % NR], s3_sem.at[t % SND], r3_sem.at[t % NR], flip(me, 2 * axes(t)[2])
        )

    def chip_sum(t, r):
        c, n = place(t)
        return acc[c, r, :, n] + hid[pl.ds(pl.multiple_of(c * half + r * rows, rows), rows), n].astype(F32)

    def store_dw(t):
        return [
            pltpu.make_async_copy(
                w.at[t % 2, :, pl.ds(h * ff, ff)], o.at[pl.ds(pl.multiple_of(t * ct, ct), ct)], out_sem.at[t % 2, h]
            )
            for h, o in ((0, dwg_hbm), (1, dwu_hbm))
        ]

    def step_b(i, _):
        @pl.when(i < tiles)
        def _():
            @pl.when(i + 1 < tiles)
            def _():
                for c in load_w(i + 1):
                    c.start()

            for c in load_w(i):
                c.wait()

            @pl.when(i >= SND)
            def _():
                c0(i - SND).wait_send()

            part = lax.dot_general(dg[0].reshape(half, 2 * ff), w[i % 2], NT, preferred_element_type=F32)
            s0[i % SND] = part.astype(BF16)

        t1, t2, t3, t4 = i - 1, i - 1 - B1, i - 1 - B1 - B2, i - LAG_B

        @pl.when((t1 >= 0) & (t1 < tiles))
        def _():
            @pl.when(t1 >= SND)
            def _():
                c1(t1 - SND).wait_send()

            c0(t1).wait_recv()
            a, b, c = axes(t1)
            for q, r in enumerate((a, a + c, a + b, a + b + c)):
                s1[t1 % SND, q] = chip_sum(t1, r).astype(BF16)

        @pl.when((t2 >= 0) & (t2 < tiles))
        def _():
            @pl.when(t2 >= SND)
            def _():
                c2(t2 - SND).wait_send()

            c1(t2).wait_recv()
            a, b, c = axes(t2)
            for q, r in enumerate((b, b + c)):
                s2[t2 % SND, q] = (chip_sum(t2, r) + r1[t2 % NR, 2 + q].astype(F32)).astype(BF16)

        @pl.when((t3 >= 0) & (t3 < tiles))
        def _():
            @pl.when(t3 >= SND)
            def _():
                c3(t3 - SND).wait_send()

            c2(t3).wait_recv()
            a, b, c = axes(t3)
            s3[t3 % SND] = (
                chip_sum(t3, c) + r1[t3 % NR, 1].astype(F32) + r2[t3 % NR, 1].astype(F32)
            ).astype(BF16)

        @pl.when((t4 >= 0) & (t4 < tiles))
        def _():
            c3(t4).wait_recv()
            total = chip_sum(t4, 0) + r1[t4 % NR, 0].astype(F32) + r2[t4 % NR, 0].astype(F32)
            dx_ref[:, cols(t4)] = (total + r3[t4 % NR].astype(F32)).astype(BF16)

            @pl.when(t4 < tiles - NR)
            def _():
                give(credit_b)

        @pl.when(i < tiles)
        def _():
            take(credit_b)
            c0(i).start()

        for copy, t in ((c1, t1), (c2, t2), (c3, t3)):
            @pl.when((t >= 0) & (t < tiles))
            def _():
                copy(t).start()

        k = jnp.where(i < tiles, i + 4, i - tiles + LAG_A)

        @pl.when((i < LAG_A - 4) | (i >= tiles))
        def _():
            gather_step(x_hbm, tiles, k)

        @pl.when(i < tiles)
        def _():
            c, n = place(i)
            part = lax.dot_general(dg[1].reshape(half, 2 * ff), w[i % 2], NT, preferred_element_type=F32)
            acc[c, :, :, n] = part.reshape(8, rows, ct)

        t = i - tiles

        @pl.when(t >= 0)
        def _():
            g = t + tiles

            @pl.when(t >= 2)
            def _():
                for c in store_dw(t - 2):
                    c.wait()

            share(g % NS).wait_recv()
            block = ag[g % NS].reshape(2 * half, ct)
            for h in range(2):
                w[t % 2, :, h * ff : (h + 1) * ff] = lax.dot_general(
                    block, dg[:, :, :, h * ff : (h + 1) * ff].reshape(2 * half, ff), TN, preferred_element_type=F32
                ).astype(BF16)
            release(g, 2 * tiles - NS)
            for c in store_dw(t):
                c.start()

        return 0

    lax.fori_loop(0, 2 * tiles, step_b, 0)
    for t in range(tiles - SND, tiles):
        for c in (c0, c1, c2, c3):
            c(t).wait_send()
    for t in (tiles - 2, tiles - 1):
        for c in store_dw(t):
            c.wait()


def mlp_backward(x, dy, gate, up, w_gate, w_up, w_down, ct=256):
    rows, d = x.shape
    n, ff = gate.shape
    tiles, nf = d // ct, ff // ct
    assert n == 16 * rows and 2 * nf == NR and tiles >= NS
    anywhere = pl.BlockSpec(memory_space=pl.ANY)
    dma, vmem = pltpu.SemaphoreType.DMA, pltpu.VMEM
    return pl.pallas_call(
        functools.partial(kernel, tiles),
        out_shape=[
            jax.ShapeDtypeStruct((rows, d), BF16),
            jax.ShapeDtypeStruct((d, ff), BF16),
            jax.ShapeDtypeStruct((d, ff), BF16),
            jax.ShapeDtypeStruct((ff, d), BF16),
        ],
        in_specs=[anywhere] * 7,
        out_specs=[pl.BlockSpec(memory_space=vmem)] + [anywhere] * 3,
        scratch_shapes=[
            vmem((NS, 2, 8, rows, ct), BF16),
            vmem((2, 8, rows, ff), F32),
            vmem((16 * rows, ff), BF16),
            vmem((2, 8, rows, 2 * ff), BF16),
            vmem((2, ct, 2 * ff), BF16),
            vmem((2, ff, ct), BF16),
            vmem((2, ff, ct), BF16),
            vmem((SND, 8 * rows, ct), BF16),
            vmem((SND, 4, rows, ct), BF16),
            vmem((SND, 2, rows, ct), BF16),
            vmem((SND, rows, ct), BF16),
            vmem((NR, 4, rows, ct), BF16),
            vmem((NR, 2, rows, ct), BF16),
            vmem((NR, rows, ct), BF16),
            dma((NS, 8)), dma((NS, 8)), dma((NS,)), dma((16, 2)), dma((2, 2)), dma((2,)), dma((2,)), dma((2, 2)),
            dma((SND,)), dma((SND,)), dma((SND,)), dma((SND,)), dma((NR,)), dma((NR,)), dma((NR,)), dma((NR,)),
            pltpu.SemaphoreType.REGULAR((4,)), pltpu.SemaphoreType.REGULAR((4,)),
        ],
        compiler_params=pltpu.CompilerParams(collective_id=0, has_side_effects=True, vmem_limit_bytes=67000000),
        cost_estimate=pl.CostEstimate(flops=12 * n * ff * d, bytes_accessed=12 * ff * d, transcendentals=0),
    )(x, dy, gate, up, w_gate, w_up, w_down)


def solution(mesh):
    rows, cols = P(("dp", "tp"), None), P("dp", "tp")
    return jax.shard_map(
        mlp_backward,
        mesh=mesh,
        in_specs=(rows, rows, cols, cols, P(None, "tp"), P(None, "tp"), P("tp", None)),
        out_specs=(rows, cols, cols, P(("dp", "tp"), None)),
        check_vma=False,
    )
```

time: 1770 us -> 474 us (0.27)
  starting transfers between devices: 700 us -> 0 us
  waiting for transfers between devices: 472 us -> 0 us
  Pallas kernels: 0 us -> 432 us
  matrix products: 404 us -> 0 us
  other arithmetic: 113 us -> 0.01 us
    dot_general x34 -> x0, starting transfers between devices: 700 us -> none  [step(): dx = jnp.dot(d_gate, w_gate.T) + jnp.dot(d_up, w_up.T)]
    pallas_call x0 -> x1, Pallas kernels: none -> 432 us  [mlp_backward(): pl.pallas_call(functools.partial(kernel, tiles), out_shape=[jax.ShapeDtyp...]
    dot_general x20 -> x0, matrix products: 404 us -> none  [the longest x3 178 us: by_group(): jnp.einsum('gta,gtb->gab', a, b, preferred_element_type=jnp.float32)]
    dot_general x34 -> x0, waiting for transfers between devices: 324 us -> none  [step(): dx = jnp.dot(d_gate, w_gate.T) + jnp.dot(d_up, w_up.T)]
    unnamed x4 -> x0, waiting for transfers between devices: 147 us -> none
    dot_general x32 -> x0, other arithmetic: 108 us -> none  [the longest x16 76.9 us: step(): dx = jnp.dot(d_gate, w_gate.T) + jnp.dot(d_up, w_up.T)]
    unnamed x10 -> x16, local copies, waits for them, and re-layouts: 50.2 us -> 40.3 us
  transfers between devices with their start and end apart: 36 -> 0, of which waited for: 20 -> 0; matrix products, arithmetic and copies ran while one was open for 32% -> 0% of each run, Pallas kernels for 0% -> 0%
where the time goes in v2:
time: 474 us; the launch traced here: 473 us
  Pallas kernels  432 us (91%)
  local copies, waits for them, and re-layouts  40.3 us (9%)
    pallas_call x1, Pallas kernels, mlp_backward(): pl.pallas_call(functools.partial(kernel, tiles), out_shape=[jax.ShapeDtyp...  432 us
    unnamed x16, local copies, waits for them, and re-layouts  40.3 us

profile of v2, /device:TPU:0, one launch (start us, length us, event | category | flops | bytes accessed | tf_op | source)
XLA Modules:
  0.0 473.4 jit_solution(631679205699233393)
XLA Ops:
  0.6 432.5 %shard_map.102 = (bf16[160,7168]{1,0:T(8,128)(2,1)}, bf16[7168,1280]{1,0:T(8,128)(2,1)}, bf16[7168,1280]{1,0:T(8,128)(2,1)}, bf16[1280,7168]{1,0:T(8,128)(2,1)}) custom-call(bf16[160,7168]{1,0:T(8,128)(2,1)} %x_hbm.1, bf16[160,7168]{1,0:T(8,128)(2,1)} %dy_hbm.1, bf16[2560,1280]{1,0:T(8,128)(2,1)} %gate_hbm.1, bf16[2560,1280]{1,0:T(8,128)(2,1)} %up_hbm.1, ...), custom_call_target="tpu_custom_call" | custom-call | flops 281857228800 | bytes 110100480 | tf_op jit(solution)/shard_map/pallas_call | solution.py:419
  433.1 3.2 copy.15
  436.3 0.0 copy-start
  436.3 0.0 slice-start
  436.3 0.0 slice-start.1
  436.3 0.0 slice-start.2
  436.3 19.7 %copy.16 = bf16[7168,1280]{1,0:T(8,128)(2,1)} copy(bf16[7168,1280]{1,0:T(8,128)(2,1)} %get-tuple-element.9) | data formatting | bytes 36700160
  456.0 0.0 copy-done
  456.0 0.0 slice-start.3
  456.0 0.0 slice-start.4
  456.0 9.3 %copy.17 = bf16[7168,1280]{1,0:T(8,128)(2,1)} copy(bf16[7168,1280]{1,0:T(8,128)(2,1)S(1)} %copy-done) | data formatting | bytes 36700160
  465.3 0.0 slice-done
  465.3 0.0 slice-done.1
  465.3 0.0 slice-done.2
  465.3 0.5 slice-done.3
  465.8 0.9 slice-done.4
  466.7 6.7 %copy.18 = bf16[1280,7168]{1,0:T(8,128)(2,1)} copy(bf16[1280,7168]{1,0:T(8,128)(2,1)S(1)} %bitcast.1) | data formatting | bytes 36700160
  (1 shorter events, 0.0 us)
Async XLA Ops:
  436.3 19.7 %copy-start = (bf16[7168,1280]{1,0:T(8,128)(2,1)S(1)}, bf16[7168,1280]{1,0:T(8,128)(2,1)}, u32[]{:S(2)}) copy-start(bf16[7168,1280]{1,0:T(8,128)(2,1)} %get-tuple-element.10) | copy-start | bytes 55050244
  436.3 29.0 %slice-start = ((s8[18350080]{0:T(1024)(128)(4,1)}), s8[4194304]{0:T(1024)(128)(4,1)S(1)}, s32[]{:S(2)}) async-start(s8[18350080]{0:T(1024)(128)(4,1)} %bitcast), calls=%async_computation | async-start | bytes 8388608
  436.3 29.0 %slice-start.1 = ((s8[18350080]{0:T(1024)(128)(4,1)}), s8[4194304]{0:T(1024)(128)(4,1)S(1)}, s32[]{:S(2)}) async-start(s8[18350080]{0:T(1024)(128)(4,1)} %bitcast), calls=%async_computation.1 | async-start | bytes 8388608
  436.3 29.0 %slice-start.2 = ((s8[18350080]{0:T(1024)(128)(4,1)}), s8[4194304]{0:T(1024)(128)(4,1)S(1)}, s32[]{:S(2)}) async-start(s8[18350080]{0:T(1024)(128)(4,1)} %bitcast), calls=%async_computation.2 | async-start | bytes 8388608
  456.0 9.8 %slice-start.3 = ((s8[18350080]{0:T(1024)(128)(4,1)}), s8[4194304]{0:T(1024)(128)(4,1)S(1)}, s32[]{:S(2)}) async-start(s8[18350080]{0:T(1024)(128)(4,1)} %bitcast), calls=%async_computation.3 | async-start | bytes 8388608
  456.0 10.7 %slice-start.4 = ((s8[18350080]{0:T(1024)(128)(4,1)}), s8[1572864]{0:T(1024)(128)(4,1)S(1)}, s32[]{:S(2)}) async-start(s8[18350080]{0:T(1024)(128)(4,1)} %bitcast), calls=%async_computation.4 | async-start | bytes 3145728

commit v3 on v2

--- a/solution.py
+++ b/solution.py
@@ -223,9 +223,10 @@
         def _():
             store_dwd(t - 2).wait()
 
-        for n in range(nf):
-            dwd[t % 2, n * ct : (n + 1) * ct, :] = lax.dot_general(
-                hid[:, n * ct : (n + 1) * ct], ag[slot].reshape(2 * half, ct), TN, preferred_element_type=F32
+        piece = ff // 2
+        for n in range(2):
+            dwd[t % 2, n * piece : (n + 1) * piece, :] = lax.dot_general(
+                hid[:, n * piece : (n + 1) * piece], ag[slot].reshape(2 * half, ct), TN, preferred_element_type=F32
             ).astype(BF16)
         release(t, 2 * tiles - NS)
         store_dwd(t).start()
@@ -360,7 +361,7 @@
             take(credit_b)
             c0(i).start()
 
-        for copy, t in ((c1, t1), (c2, t2), (c3, t3)):
+        for copy, t in ((c3, t3), (c2, t2), (c1, t1)):
             @pl.when((t >= 0) & (t < tiles))
             def _():
                 copy(t).start()

time: 474 us -> 454 us (0.958)
  Pallas kernels: 432 us -> 412 us
    pallas_call x1, Pallas kernels: 432 us -> 412 us  [mlp_backward(): pl.pallas_call(functools.partial(kernel, tiles), out_shape=[jax.ShapeDtyp...]
where the time goes in v3:
time: 454 us; the launch traced here: 453 us
  Pallas kernels  412 us (91%)
  local copies, waits for them, and re-layouts  40.3 us (9%)
    pallas_call x1, Pallas kernels, mlp_backward(): pl.pallas_call(functools.partial(kernel, tiles), out_shape=[jax.ShapeDtyp...  412 us
    unnamed x16, local copies, waits for them, and re-layouts  40.3 us

profile of v3, /device:TPU:0, one launch (start us, length us, event | category | flops | bytes accessed | tf_op | source)
XLA Modules:
  0.0 453.4 jit_solution(10208452152063119093)
XLA Ops:
  0.6 412.5 %shard_map.102 = (bf16[160,7168]{1,0:T(8,128)(2,1)}, bf16[7168,1280]{1,0:T(8,128)(2,1)}, bf16[7168,1280]{1,0:T(8,128)(2,1)}, bf16[1280,7168]{1,0:T(8,128)(2,1)}) custom-call(bf16[160,7168]{1,0:T(8,128)(2,1)} %x_hbm.1, bf16[160,7168]{1,0:T(8,128)(2,1)} %dy_hbm.1, bf16[2560,1280]{1,0:T(8,128)(2,1)} %gate_hbm.1, bf16[2560,1280]{1,0:T(8,128)(2,1)} %up_hbm.1, ...), custom_call_target="tpu_custom_call" | custom-call | flops 281857228800 | bytes 110100480 | tf_op jit(solution)/shard_map/pallas_call | solution.py:420
  413.1 3.2 copy.15
  416.3 0.0 copy-start
  416.3 0.0 slice-start
  416.3 0.0 slice-start.1
  416.3 0.0 slice-start.2
  416.3 19.7 %copy.16 = bf16[7168,1280]{1,0:T(8,128)(2,1)} copy(bf16[7168,1280]{1,0:T(8,128)(2,1)} %get-tuple-element.9) | data formatting | bytes 36700160
  436.0 0.0 copy-done
  436.0 0.0 slice-start.3
  436.0 0.0 slice-start.4
  436.0 9.3 %copy.17 = bf16[7168,1280]{1,0:T(8,128)(2,1)} copy(bf16[7168,1280]{1,0:T(8,128)(2,1)S(1)} %copy-done) | data formatting | bytes 36700160
  445.3 0.0 slice-done
  445.3 0.0 slice-done.1
  445.3 0.0 slice-done.2
  445.3 0.5 slice-done.3
  445.8 0.9 slice-done.4
  446.7 6.7 %copy.18 = bf16[1280,7168]{1,0:T(8,128)(2,1)} copy(bf16[1280,7168]{1,0:T(8,128)(2,1)S(1)} %bitcast.1) | data formatting | bytes 36700160
  (1 shorter events, 0.0 us)
Async XLA Ops:
  416.3 19.7 %copy-start = (bf16[7168,1280]{1,0:T(8,128)(2,1)S(1)}, bf16[7168,1280]{1,0:T(8,128)(2,1)}, u32[]{:S(2)}) copy-start(bf16[7168,1280]{1,0:T(8,128)(2,1)} %get-tuple-element.10) | copy-start | bytes 55050244
  416.3 29.0 %slice-start = ((s8[18350080]{0:T(1024)(128)(4,1)}), s8[4194304]{0:T(1024)(128)(4,1)S(1)}, s32[]{:S(2)}) async-start(s8[18350080]{0:T(1024)(128)(4,1)} %bitcast), calls=%async_computation | async-start | bytes 8388608
  416.3 29.0 %slice-start.1 = ((s8[18350080]{0:T(1024)(128)(4,1)}), s8[4194304]{0:T(1024)(128)(4,1)S(1)}, s32[]{:S(2)}) async-start(s8[18350080]{0:T(1024)(128)(4,1)} %bitcast), calls=%async_computation.1 | async-start | bytes 8388608
  416.3 29.0 %slice-start.2 = ((s8[18350080]{0:T(1024)(128)(4,1)}), s8[4194304]{0:T(1024)(128)(4,1)S(1)}, s32[]{:S(2)}) async-start(s8[18350080]{0:T(1024)(128)(4,1)} %bitcast), calls=%async_computation.2 | async-start | bytes 8388608
  436.0 9.8 %slice-start.3 = ((s8[18350080]{0:T(1024)(128)(4,1)}), s8[4194304]{0:T(1024)(128)(4,1)S(1)}, s32[]{:S(2)}) async-start(s8[18350080]{0:T(1024)(128)(4,1)} %bitcast), calls=%async_computation.3 | async-start | bytes 8388608
  436.0 10.7 %slice-start.4 = ((s8[18350080]{0:T(1024)(128)(4,1)}), s8[1572864]{0:T(1024)(128)(4,1)S(1)}, s32[]{:S(2)}) async-start(s8[18350080]{0:T(1024)(128)(4,1)} %bitcast), calls=%async_computation.4 | async-start | bytes 3145728
